TPU v7x, 512 devices: a whole 4x4x16 slice. The times are simulated.
512 devices in a mesh: dom: 128 (over z, y, core), level: 4 (over x).
Axes of the slice: x: 4, y: 4, z: 16, core: 2. Of those that a mesh axis runs over, the one named last changes fastest.
Arguments:
- dg_values: bfloat16 [1572864, 384], P(('dom', 'level')), may hold values from -6 to 6
- stiff_mu: bfloat16 [384, 384], replicated, may hold values from -0.1 to 2, as said below
- stiff_lam: bfloat16 [384, 384], replicated, may hold values from -0.1 to 2, as said below
- coef_mu: float32 [1572864], P(('dom', 'level')), may hold values from 0.25 to 4
- coef_lam: float32 [1572864], P(('dom', 'level')), may hold values from 0.25 to 4
- elem_count: int32 [512], P(('dom', 'level')), may hold values from 384 to 3072, as said below
- elem_block: int32 [3, 1572864], P(None, ('dom', 'level')), may hold values from 0 to 1023
- share_map: int32 [512, 8, 32], P(('dom', 'level')), may hold values from 0 to 1024, as said below
- hang_child: int32 [512, 64], P(('dom', 'level')), may hold values from 0 to 1024, as said below
- hang_parent: int32 [512, 64, 2], P(('dom', 'level')), may hold values from 0 to 1023
Outputs:
- projected: float32 [3, 524288, 128], P(None, ('dom', 'level'))
- energy: float32 [], replicated
Inputs may be any that keep to these rules, and one draw needn't show every extreme that they name: `elem_count`: between 384 and 3072; one device, drawn anew, holds exactly 3072. `share_map`: Slots agree in pairs: [d, o, s] is live exactly when the partner's [d2, o', s] is live, and they name the same DoF block. Slots toward ranks outside 0 to 127 are empty. For every offset some rank pair fills all 32 slots. `hang_child`: on each device of level index 1 or more, 64 distinct blocks below 1024; on devices of level index 0 every entry is 1024 (no hanging blocks). `hang_parent`: block numbers on the device of the same rank and the next lower level index; unused on level index 0. `stiff_mu`: Symmetric. `stiff_lam`: Symmetric.
All inputs are finite; a program needn't handle non-finite values.
Results may differ from a plain program's by a relative error of at most 0.0003.
Values sent between devices are 32-bit elements; how exact they have to be, the bound alone decides.
A program may use at most 64 MiB of HBM per device.

v0:
```python
import functools

import jax
import jax.numpy as jnp
from jax import lax
from jax.sharding import Mesh
from jax.sharding import PartitionSpec as P

DOM = ("dom_0", "dom_1", "dom_2")
DOM_LEVEL = ("dom_0", "dom_1", "dom_2", "level")


def from_behind(block, axis, distance):
    devices = range(lax.axis_size(axis))
    route = [(i - distance, i) for i in devices if i - distance in devices]
    return lax.ppermute(block, axis, route)


def by_axis(x, axes):
    return functools.reduce(lax.psum, axes, x)


def shards(
    dg_values,
    stiff_mu,
    stiff_lam,
    coef_mu,
    coef_lam,
    elem_count,
    elem_block,
    share_map,
    hang_child,
    hang_parent,
):
    elements = dg_values.shape[0]
    row_width = stiff_mu.shape[0]
    block_size = row_width // 3
    block_count = elements // 3
    offsets_half = share_map.shape[1] // 2
    joined = jnp.concatenate((stiff_mu, stiff_lam), axis=1)
    product = jnp.dot(dg_values, joined, preferred_element_type=jnp.float32)
    forces = coef_mu[:, None] * product[:, :row_width] + coef_lam[:, None] * product[:, row_width:]
    live_rows = jnp.arange(elements) < elem_count[0]
    forces = jnp.where(live_rows[:, None], forces, jnp.float32(0.0))
    energy_part = 0.5 * jnp.sum(dg_values.astype(jnp.float32) * forces)
    component_forces = jnp.transpose(forces.reshape(elements, 3, block_size), (1, 0, 2))
    block_ids = jnp.arange(block_count + 1, dtype=jnp.int32)

    def sum_blocks(packed):
        target_ids, component_part = packed
        selector = (block_ids[:, None] == target_ids[None, :]).astype(jnp.float32)
        return jnp.dot(
            selector,
            component_part,
            precision=lax.Precision.HIGHEST,
            preferred_element_type=jnp.float32,
        )

    local_blocks = lax.map(sum_blocks, (elem_block, component_forces))
    slot_blocks = share_map[0]
    outgoing = jnp.transpose(local_blocks[:, slot_blocks, :], (1, 0, 2, 3))
    offsets = [step + 1 for step in range(offsets_half)] + [
        -(step + 1) for step in range(offsets_half)
    ]
    pieces = [None] * (2 * offsets_half)
    for slot_index in range(2 * offsets_half):
        opposite = (slot_index + offsets_half) % (2 * offsets_half)
        pieces[opposite] = from_behind(outgoing[slot_index], DOM, offsets[slot_index])
    incoming = jnp.stack(pieces)
    received = jnp.transpose(incoming, (1, 0, 2, 3)).reshape(3, -1, block_size)
    assembled = local_blocks.at[:, slot_blocks.reshape(-1), :].add(received)
    wanted = from_behind(hang_parent, "level", -1)
    chosen = assembled[:, wanted[0].reshape(-1), :]
    picked = from_behind(chosen, "level", 1)
    parent_pairs = picked.reshape(3, -1, 2, block_size)
    child_values = 0.5 * (parent_pairs[:, :, 0] + parent_pairs[:, :, 1])
    projected = assembled.at[:, hang_child[0], :].set(child_values)
    scale_total = jnp.float32(row_width * elements * lax.axis_size(DOM) * lax.axis_size("level"))
    energy = by_axis(energy_part, DOM_LEVEL) / scale_total
    return (projected[:, :block_count], energy)


def solution(mesh):
    finer = Mesh(
        mesh.devices.reshape(16, 4, 2, mesh.shape["level"]), ("dom_0", "dom_1", "dom_2", "level")
    )
    placed = (
        P(DOM_LEVEL, None),
        P(),
        P(),
        P(DOM_LEVEL),
        P(DOM_LEVEL),
        P(DOM_LEVEL),
        P(None, DOM_LEVEL),
        P(DOM_LEVEL, None, None),
        P(DOM_LEVEL, None),
        P(DOM_LEVEL, None, None),
    )
    return jax.shard_map(
        shards,
        mesh=finer,
        in_specs=placed,
        out_specs=(P(None, DOM_LEVEL, None), P()),
        check_vma=False,
    )
```

profile of v0, /device:TPU:1, one launch (start us, length us, event | category | flops | bytes accessed | tf_op | source)
XLA Modules:
  0.0 209.7 jit_solution(11319202221531676949)
XLA Ops:
  0.6 1.3 collective-permute-start.8
  1.9 0.0 copy-start
  2.0 0.0 copy-start.3
  2.0 0.0 copy-start.4
  2.0 4.5 %copy.33 = bf16[3072,384]{0,1:T(8,128)(2,1)} copy(bf16[3072,384]{1,0:T(8,128)(2,1)} %param.12) | data formatting | bytes 4718592 | tf_op args[0]
  7.1 0.0 copy-done
  7.1 0.0 copy-done.3
  7.1 0.0 copy-done.4
  7.1 0.0 copy-start.1
  7.1 0.0 copy-start.6
  7.1 0.0 copy-start.7
  7.2 2.7 %convolution_bitcast_fusion = f32[3072,768]{0,1:T(8,128)S(1)} fusion(bf16[3072,384]{1,0:T(8,128)(2,1)S(1)} %copy-done, bf16[384,384]{1,0:T(8,128)(2,1)S(1)} %copy-done.3, bf16[384,384]{1,0:T(8,128)(2,1)S(1)} %copy-done.4), kind=kOutput, calls=%fused_computation.13 | convolution fusion | flops 1813118976 | bytes 12386304 | tf_op jit(solution)/shard_map/dot_general | solution.py:41
  9.8 0.0 copy-done.1
  9.8 4.4 %multiply_reduce_fusion = (f32[]{:T(128)}, f32[3072,384]{0,1:T(8,128)}) fusion(bf16[3072,384]{0,1:T(8,128)(2,1)S(1)} %copy-done.1, f32[3072,768]{0,1:T(8,128)S(1)} %convolution_bitcast_fusion, f32[3072]{0:T(1024)S(1)} %copy-done.6, f32[3072]{0:T(1024)S(1)} %copy-done.7, pred[3072]{0:T(1024)(128)(4,1)S(1)} %iota_compare_fusion.4), kind=kLoop, calls=%fused_computation.18 | loop fusion | flops 8257535 | bytes 16542724 | tf_op jit(solution)/shard_map/reduce_sum | solution.py:45
  14.3 6.2 %copy.27 = f32[3072,3,128]{2,0,1:T(8,128)} copy(f32[3072,3,128]{0,2,1:T(8,128)} %bitcast.88) | data formatting | bytes 9437184 | tf_op jit(solution)/shard_map/reshape | solution.py:46
  21.1 31.0 %psum.28 = f32[]{:T(128)} all-reduce(f32[]{:T(128)S(6)} %mul.39), channel_id=1, replica_groups=mesh['dom_0'=16,'dom_1'=4,'dom_2'=2,'level'=4] {'dom_0'}, use_global_device_ids=true, to_apply=%region_5.6 | all-reduce | flops 1 | bytes 8 | tf_op jit(solution)/shard_map/psum | solution.py:20
  52.2 0.0 copy-done.2
  52.2 73.7 %while.11 = (s32[]{:T(128)}, f32[3,1025,128]{2,0,1:T(4,128)S(1)}, s32[3,3072]{1,0:T(4,128)}, f32[3,3072,128]{2,1,0:T(8,128)}, s32[]{:T(128)}, /*index=5*/s32[]{:T(128)}) while((s32[]{:T(128)}, f32[3,1025,128]{2,0,1:T(4,128)S(1)}, s32[3,3072]{1,0:T(4,128)}, f32[3,3072,128]{2,1,0:T(8,128)}, s32[]{:T(128)}, /*index=5*/s32[]{:T(128)}) %tuple.40), condition=%wide.region_1.2_spmd.clone, body=%wide.region_0.1_spmd.clone.sunk | while | flops 4839705600 | bytes 4234317 | solution.py:59
  52.2 0.8 constant_dynamic-slice_fusion.2
  53.0 7.2 %fusion.24 = f32[1,1025,128]{2,1,0:T(8,128)S(1)} fusion(s32[3072]{0:T(1024)S(1)} %bitcast.92, f32[3,3072,128]{2,1,0:T(8,128)} %get-tuple-element.104, s32[]{:T(128)} %get-tuple-element.95), kind=kOutput, calls=%fused_computation.8.clone.1 | convolution fusion | flops 4839705600 | bytes 2110464 | tf_op jit(solution)/shard_map/while/body/eval_jaxpr/dot_general | solution.py:52
  60.2 3.3 %copy.41 = f32[1,1025,128]{2,0,1:T(1,128)S(1)} copy(f32[1,1025,128]{2,1,0:T(8,128)S(1)} %fusion.24) | data formatting | bytes 1049600 | tf_op jit(solution)/shard_map/while/body/jit(dynamic_update_index_in_dim)/dynamic_update_slice | solution.py:59
  63.5 13.2 %dynamic_update_slice.6 = f32[3,1025,128]{2,0,1:T(4,128)S(1)} dynamic-update-slice(f32[3,1025,128]{2,0,1:T(4,128)S(1)} %get-tuple-element.96, f32[1,1025,128]{2,0,1:T(1,128)S(1)} %copy.41, s32[]{:T(128)} %get-tuple-element.95, s32[]{:T(128)} %constant.11.clone.1..sunk, s32[]{:T(128)} %constant.11.clone.1..sunk) | dynamic-update-slice | bytes 1049604 | tf_op jit(solution)/shard_map/while/body/jit(dynamic_update_index_in_dim)/dynamic_update_slice | solution.py:59
  76.7 0.8 constant_dynamic-slice_fusion.2
  77.6 7.2 %fusion.24 = f32[1,1025,128]{2,1,0:T(8,128)S(1)} fusion(s32[3072]{0:T(1024)S(1)} %bitcast.92, f32[3,3072,128]{2,1,0:T(8,128)} %get-tuple-element.104, s32[]{:T(128)} %get-tuple-element.95), kind=kOutput, calls=%fused_computation.8.clone.1 | convolution fusion | flops 4839705600 | bytes 2110464 | tf_op jit(solution)/shard_map/while/body/eval_jaxpr/dot_general | solution.py:52
  84.7 3.3 %copy.41 = f32[1,1025,128]{2,0,1:T(1,128)S(1)} copy(f32[1,1025,128]{2,1,0:T(8,128)S(1)} %fusion.24) | data formatting | bytes 1049600 | tf_op jit(solution)/shard_map/while/body/jit(dynamic_update_index_in_dim)/dynamic_update_slice | solution.py:59
  88.0 13.2 %dynamic_update_slice.6 = f32[3,1025,128]{2,0,1:T(4,128)S(1)} dynamic-update-slice(f32[3,1025,128]{2,0,1:T(4,128)S(1)} %get-tuple-element.96, f32[1,1025,128]{2,0,1:T(1,128)S(1)} %copy.41, s32[]{:T(128)} %get-tuple-element.95, s32[]{:T(128)} %constant.11.clone.1..sunk, s32[]{:T(128)} %constant.11.clone.1..sunk) | dynamic-update-slice | bytes 1049604 | tf_op jit(solution)/shard_map/while/body/jit(dynamic_update_index_in_dim)/dynamic_update_slice | solution.py:59
  101.3 0.8 constant_dynamic-slice_fusion.2
  102.1 7.2 %fusion.24 = f32[1,1025,128]{2,1,0:T(8,128)S(1)} fusion(s32[3072]{0:T(1024)S(1)} %bitcast.92, f32[3,3072,128]{2,1,0:T(8,128)} %get-tuple-element.104, s32[]{:T(128)} %get-tuple-element.95), kind=kOutput, calls=%fused_computation.8.clone.1 | convolution fusion | flops 4839705600 | bytes 2110464 | tf_op jit(solution)/shard_map/while/body/eval_jaxpr/dot_general | solution.py:52
  109.3 3.3 %copy.41 = f32[1,1025,128]{2,0,1:T(1,128)S(1)} copy(f32[1,1025,128]{2,1,0:T(8,128)S(1)} %fusion.24) | data formatting | bytes 1049600 | tf_op jit(solution)/shard_map/while/body/jit(dynamic_update_index_in_dim)/dynamic_update_slice | solution.py:59
  112.6 13.2 %dynamic_update_slice.6 = f32[3,1025,128]{2,0,1:T(4,128)S(1)} dynamic-update-slice(f32[3,1025,128]{2,0,1:T(4,128)S(1)} %get-tuple-element.96, f32[1,1025,128]{2,0,1:T(1,128)S(1)} %copy.41, s32[]{:T(128)} %get-tuple-element.95, s32[]{:T(128)} %constant.11.clone.1..sunk, s32[]{:T(128)} %constant.11.clone.1..sunk) | dynamic-update-slice | bytes 1049604 | tf_op jit(solution)/shard_map/while/body/jit(dynamic_update_index_in_dim)/dynamic_update_slice | solution.py:59
  125.8 0.0 copy-start.8
  125.9 9.4 %psum.29 = f32[]{:T(128)} all-reduce(f32[]{:T(128)} %psum.28), channel_id=1, replica_groups=mesh['dom_0'=16,'dom_1'=4,'dom_2'=2,'level'=4] {'dom_1'}, use_global_device_ids=true, to_apply=%region_6.7 | all-reduce | flops 1 | bytes 8 | tf_op jit(solution)/shard_map/psum | solution.py:20
  135.2 12.4 %psum.30 = f32[]{:T(128)} all-reduce(f32[]{:T(128)} %psum.29), channel_id=1, replica_groups=mesh['dom_0'=16,'dom_1'=4,'dom_2'=2,'level'=4] {'dom_2'}, use_global_device_ids=true, to_apply=%region_7.8 | all-reduce | flops 1 | bytes 8 | tf_op jit(solution)/shard_map/psum | solution.py:20
  147.7 0.1 reshape_squeeze.6
  147.7 0.1 reshape.140
  147.8 0.0 collective-permute-done.8
  147.8 0.1 copy.30
  147.9 0.1 reshape_squeeze.7
  148.1 1.0 gather_fusion
  149.1 0.1 slice_bitcast_fusion.2
  149.2 2.3 %collective-permute-start = (f32[3,32,128]{2,0,1:T(4,128)S(1)}, f32[3,32,128]{2,0,1:T(4,128)S(1)}, u32[]{:S(2)}, u32[]{:S(2)}) collective-permute-start(f32[3,32,128]{2,0,1:T(4,128)S(1)} %get-tuple-element.61), channel_id=1, source_target_pairs={{4,0},{8,4},{12,8},{16,12},{20,16},{24,20},{28,24},{32,28},{36,32}... | collective-permute-start | bytes 147464 | tf_op jit(solution)/shard_map/ppermute | solution.py:16
  151.4 10.7 %psum.31 = f32[]{:T(128)} all-reduce(f32[]{:T(128)} %psum.30), channel_id=1, replica_groups=mesh['dom_0'=16,'dom_1'=4,'dom_2'=2,'level'=4] {'level'}, use_global_device_ids=true, to_apply=%region_8.9 | all-reduce | flops 1 | bytes 8 | tf_op jit(solution)/shard_map/psum | solution.py:20
  162.8 1.3 collective-permute-start.1
  164.1 1.3 collective-permute-start.2
  165.4 1.3 collective-permute-start.3
  166.7 5.8 %collective-permute-start.4 = (f32[3,32,128]{2,0,1:T(4,128)S(1)}, f32[3,32,128]{2,0,1:T(4,128)S(1)}, u32[]{:S(2)}, u32[]{:S(2)}) collective-permute-start(f32[3,32,128]{2,0,1:T(4,128)S(1)} %get-tuple-element.57), channel_id=1, source_target_pairs={{0,4},{4,8},{8,12},{12,16},{16,20},{20,24},{24,28},{28,32},{32,36}... | collective-permute-start | bytes 147464 | tf_op jit(solution)/shard_map/ppermute | solution.py:16
  172.5 0.0 collective-permute-done
  172.5 4.9 %collective-permute-start.5 = (f32[3,32,128]{2,0,1:T(4,128)S(1)}, f32[3,32,128]{2,0,1:T(4,128)S(1)}, u32[]{:S(2)}, u32[]{:S(2)}) collective-permute-start(f32[3,32,128]{2,0,1:T(4,128)S(1)} %get-tuple-element.56), channel_id=1, source_target_pairs={{0,8},{4,12},{8,16},{12,20},{16,24},{20,28},{24,32},{28,36},{32,40... | collective-permute-start | bytes 147464 | tf_op jit(solution)/shard_map/ppermute | solution.py:16
  177.5 0.0 collective-permute-done.1
  177.5 4.4 %collective-permute-start.6 = (f32[3,32,128]{2,0,1:T(4,128)S(1)}, f32[3,32,128]{2,0,1:T(4,128)S(1)}, u32[]{:S(2)}, u32[]{:S(2)}) collective-permute-start(f32[3,32,128]{2,0,1:T(4,128)S(1)} %get-tuple-element.55), channel_id=1, source_target_pairs={{0,12},{4,16},{8,20},{12,24},{16,28},{20,32},{24,36},{28,40},{32,4... | collective-permute-start | bytes 147464 | tf_op jit(solution)/shard_map/ppermute | solution.py:16
  181.9 0.0 collective-permute-done.2
  181.9 5.2 %collective-permute-start.7 = (f32[3,32,128]{2,0,1:T(4,128)S(1)}, f32[3,32,128]{2,0,1:T(4,128)S(1)}, u32[]{:S(2)}, u32[]{:S(2)}) collective-permute-start(f32[3,32,128]{2,0,1:T(4,128)S(1)} %get-tuple-element.54), channel_id=1, source_target_pairs={{0,16},{4,20},{8,24},{12,28},{16,32},{20,36},{24,40},{28,44},{32,4... | collective-permute-start | bytes 147464 | tf_op jit(solution)/shard_map/ppermute | solution.py:16
  187.1 0.0 collective-permute-done.3
  187.1 0.0 collective-permute-done.4
  187.1 0.0 collective-permute-done.5
  187.2 0.0 collective-permute-done.6
  187.2 1.1 collective-permute-done.7
  188.4 9.0 %scatter_fusion = f32[3,1025,128]{2,0,1:T(4,128)S(1)} fusion(f32[3,1025,128]{2,0,1:T(4,128)S(1)} %get-tuple-element.29, s32[256]{0:T(256)S(1)} %bitcast.95, f32[256,3,128]{2,1,0:T(4,128)S(1)} %bitcast.91), kind=kCustom, calls=%fused_computation.2 | custom fusion | flops 98304 | bytes 1180672 | tf_op jit(solution)/shard_map/scatter-add | solution.py:71
  197.3 0.7 gather_fusion.1
  198.1 1.3 collective-permute-start.9
  199.4 4.9 %collective-permute-done.9 = f32[3,128,128]{2,0,1:T(4,128)S(1)} collective-permute-done((f32[3,128,128]{2,0,1:T(4,128)S(1)}, f32[3,128,128]{2,0,1:T(4,128)S(1)}, u32[]{:S(2)}, u32[]{:S(2)}) %collective-permute-start.9) | collective-permute-done | bytes 196640 | tf_op jit(solution)/shard_map/ppermute | solution.py:16
  204.3 2.6 %scatter_fusion.1 = f32[3,1025,128]{2,0,1:T(4,128)S(1)} fusion(f32[3,1025,128]{2,0,1:T(4,128)S(1)} %scatter_fusion, s32[64]{0:T(128)S(1)} %fusion.16, f32[64,3,128]{2,1,0:T(4,128)S(1)} %fusion.15), kind=kCustom, calls=%fused_computation.3 | custom fusion | bytes 295168 | tf_op jit(solution)/shard_map/scatter | solution.py:77
  206.9 0.4 slice.68
  207.3 1.2 copy.34
  (22 shorter events, 0.2 us)
Async XLA Ops:
  0.6 147.2 %collective-permute-start.8 = (s32[1,64,2]{1,2,0:T(2,128)}, s32[1,64,2]{1,2,0:T(2,128)S(1)}, u32[]{:S(2)}, u32[]{:S(2)}) collective-permute-start(s32[1,64,2]{1,2,0:T(2,128)} %param.21), channel_id=1, source_target_pairs={{1,0},{2,1},{3,2},{5,4},{6,5},{7,6},{9,8},{10,9},{11,10},{13,12},{... | collective-permute-start | bytes 1544 | tf_op jit(solution)/shard_map/ppermute | solution.py:16
  1.9 5.2 %copy-start = (bf16[3072,384]{1,0:T(8,128)(2,1)S(1)}, bf16[3072,384]{1,0:T(8,128)(2,1)}, u32[]{:S(2)}) copy-start(bf16[3072,384]{1,0:T(8,128)(2,1)} %param.12) | copy-start | bytes 7077892
  2.0 5.2 %copy-start.3 = (bf16[384,384]{1,0:T(8,128)(2,1)S(1)}, bf16[384,384]{1,0:T(8,128)(2,1)}, u32[]{:S(2)}) copy-start(bf16[384,384]{1,0:T(8,128)(2,1)} %param.14) | copy-start | bytes 884740
  2.0 5.2 %copy-start.4 = (bf16[384,384]{1,0:T(8,128)(2,1)S(1)}, bf16[384,384]{1,0:T(8,128)(2,1)}, u32[]{:S(2)}) copy-start(bf16[384,384]{1,0:T(8,128)(2,1)} %param.13) | copy-start | bytes 884740
  7.1 2.7 %copy-start.1 = (bf16[3072,384]{0,1:T(8,128)(2,1)S(1)}, bf16[3072,384]{0,1:T(8,128)(2,1)}, u32[]{:S(2)}) copy-start(bf16[3072,384]{0,1:T(8,128)(2,1)} %copy.33) | copy-start | bytes 7077892
  7.1 2.7 %copy-start.6 = (f32[3072]{0:T(1024)S(1)}, f32[3072]{0:T(1024)}, u32[]{:S(2)}) copy-start(f32[3072]{0:T(1024)} %param.16) | copy-start | bytes 36868
  7.1 2.7 %copy-start.7 = (f32[3072]{0:T(1024)S(1)}, f32[3072]{0:T(1024)}, u32[]{:S(2)}) copy-start(f32[3072]{0:T(1024)} %param.15) | copy-start | bytes 36868
  14.3 37.9 %copy-start.2 = (f32[3,1025,128]{2,0,1:T(4,128)S(1)}, f32[3,1025,128]{2,0,1:T(4,128)}, u32[]{:S(2)}) copy-start(f32[3,1025,128]{2,0,1:T(4,128)} %custom-call.5) | copy-start | bytes 4723204
  52.2 83.1 %copy-start.5 = (s32[1,8,32]{2,1,0:T(8,128)S(1)}, s32[1,8,32]{2,1,0:T(8,128)}, u32[]{:S(2)}) copy-start(s32[1,8,32]{2,1,0:T(8,128)} %param.19) | copy-start | bytes 3076
  125.8 73.5 %copy-start.8 = (s32[1,64]{1,0:T(1,128)S(1)}, s32[1,64]{1,0:T(1,128)}, u32[]{:S(2)}) copy-start(s32[1,64]{1,0:T(1,128)} %param.20) | copy-start | bytes 772
  149.2 23.3 %collective-permute-start = (f32[3,32,128]{2,0,1:T(4,128)S(1)}, f32[3,32,128]{2,0,1:T(4,128)S(1)}, u32[]{:S(2)}, u32[]{:S(2)}) collective-permute-start(f32[3,32,128]{2,0,1:T(4,128)S(1)} %get-tuple-element.61), channel_id=1, source_target_pairs={{4,0},{8,4},{12,8},{16,12},{20,16},{24,20},{28,24},{32,28},{36,32}... | collective-permute-start | bytes 147464 | tf_op jit(solution)/shard_map/ppermute | solution.py:16
  162.8 14.7 %collective-permute-start.1 = (f32[3,32,128]{2,0,1:T(4,128)S(1)}, f32[3,32,128]{2,0,1:T(4,128)S(1)}, u32[]{:S(2)}, u32[]{:S(2)}) collective-permute-start(f32[3,32,128]{2,0,1:T(4,128)S(1)} %get-tuple-element.60), channel_id=1, source_target_pairs={{8,0},{12,4},{16,8},{20,12},{24,16},{28,20},{32,24},{36,28},{40,32... | collective-permute-start | bytes 147464 | tf_op jit(solution)/shard_map/ppermute | solution.py:16
  164.1 17.8 %collective-permute-start.2 = (f32[3,32,128]{2,0,1:T(4,128)S(1)}, f32[3,32,128]{2,0,1:T(4,128)S(1)}, u32[]{:S(2)}, u32[]{:S(2)}) collective-permute-start(f32[3,32,128]{2,0,1:T(4,128)S(1)} %get-tuple-element.59), channel_id=1, source_target_pairs={{12,0},{16,4},{20,8},{24,12},{28,16},{32,20},{36,24},{40,28},{44,3... | collective-permute-start | bytes 147464 | tf_op jit(solution)/shard_map/ppermute | solution.py:16
  165.4 21.7 %collective-permute-start.3 = (f32[3,32,128]{2,0,1:T(4,128)S(1)}, f32[3,32,128]{2,0,1:T(4,128)S(1)}, u32[]{:S(2)}, u32[]{:S(2)}) collective-permute-start(f32[3,32,128]{2,0,1:T(4,128)S(1)} %get-tuple-element.58), channel_id=1, source_target_pairs={{16,0},{20,4},{24,8},{28,12},{32,16},{36,20},{40,24},{44,28},{48,3... | collective-permute-start | bytes 147464 | tf_op jit(solution)/shard_map/ppermute | solution.py:16
  166.7 20.4 %collective-permute-start.4 = (f32[3,32,128]{2,0,1:T(4,128)S(1)}, f32[3,32,128]{2,0,1:T(4,128)S(1)}, u32[]{:S(2)}, u32[]{:S(2)}) collective-permute-start(f32[3,32,128]{2,0,1:T(4,128)S(1)} %get-tuple-element.57), channel_id=1, source_target_pairs={{0,4},{4,8},{8,12},{12,16},{16,20},{20,24},{24,28},{28,32},{32,36}... | collective-permute-start | bytes 147464 | tf_op jit(solution)/shard_map/ppermute | solution.py:16
  172.5 14.6 %collective-permute-start.5 = (f32[3,32,128]{2,0,1:T(4,128)S(1)}, f32[3,32,128]{2,0,1:T(4,128)S(1)}, u32[]{:S(2)}, u32[]{:S(2)}) collective-permute-start(f32[3,32,128]{2,0,1:T(4,128)S(1)} %get-tuple-element.56), channel_id=1, source_target_pairs={{0,8},{4,12},{8,16},{12,20},{16,24},{20,28},{24,32},{28,36},{32,40... | collective-permute-start | bytes 147464 | tf_op jit(solution)/shard_map/ppermute | solution.py:16
  177.5 9.7 %collective-permute-start.6 = (f32[3,32,128]{2,0,1:T(4,128)S(1)}, f32[3,32,128]{2,0,1:T(4,128)S(1)}, u32[]{:S(2)}, u32[]{:S(2)}) collective-permute-start(f32[3,32,128]{2,0,1:T(4,128)S(1)} %get-tuple-element.55), channel_id=1, source_target_pairs={{0,12},{4,16},{8,20},{12,24},{16,28},{20,32},{24,36},{28,40},{32,4... | collective-permute-start | bytes 147464 | tf_op jit(solution)/shard_map/ppermute | solution.py:16
  181.9 6.5 %collective-permute-start.7 = (f32[3,32,128]{2,0,1:T(4,128)S(1)}, f32[3,32,128]{2,0,1:T(4,128)S(1)}, u32[]{:S(2)}, u32[]{:S(2)}) collective-permute-start(f32[3,32,128]{2,0,1:T(4,128)S(1)} %get-tuple-element.54), channel_id=1, source_target_pairs={{0,16},{4,20},{8,24},{12,28},{16,32},{20,36},{24,40},{28,44},{32,4... | collective-permute-start | bytes 147464 | tf_op jit(solution)/shard_map/ppermute | solution.py:16
  198.1 6.2 %collective-permute-start.9 = (f32[3,128,128]{2,0,1:T(4,128)S(1)}, f32[3,128,128]{2,0,1:T(4,128)S(1)}, u32[]{:S(2)}, u32[]{:S(2)}) collective-permute-start(f32[3,128,128]{2,0,1:T(4,128)S(1)} %bitcast.94), channel_id=1, source_target_pairs={{0,1},{1,2},{2,3},{4,5},{5,6},{6,7},{8,9},{9,10},{10,11},{12,13},{... | collective-permute-start | bytes 589832 | tf_op jit(solution)/shard_map/ppermute | solution.py:16
where the time goes:
time: 213 us; the launch traced here: 210 us
  local copies, waits for them, and re-layouts  69.3 us (33%)
  blocking collectives  63.5 us (30%)
  starting transfers between devices  29 us (14%)
  matrix products  24.2 us (11%)
  other arithmetic  13.5 us (6%)
  waiting for transfers between devices  6.04 us (3%)
  between operations  4.11 us (2%)
    psum x4, blocking collectives, by_axis(): return functools.reduce(lax.psum, axes, x)  63.5 us
    dynamic_update_slice x6, local copies, waits for them, and re-layouts, shards(): local_blocks = lax.map(sum_blocks, (elem_block, component_forces))  49.6 us
    ppermute x10, starting transfers between devices, from_behind(): return lax.ppermute(block, axis, route)  29 us
    dot_general x3, matrix products, sum_blocks(): jnp.dot(selector, component_part, precision=lax.Precision.HIGHEST, prefer...  21.6 us
    scatter-add x1, other arithmetic, shards(): assembled = local_blocks.at[:, slot_blocks.reshape(-1), :].add(received)  8.95 us
    reshape x1, local copies, waits for them, and re-layouts, shards(): forces.reshape(elements, 3, block_size)  6.19 us
    ppermute x10, waiting for transfers between devices, from_behind(): return lax.ppermute(block, axis, route)  6.04 us
    unnamed x27, local copies, waits for them, and re-layouts  5.88 us
  transfers between devices with their start and end apart: 10, of which 2 were waited for; matrix products, arithmetic and copies ran while one was open for 44% of the time, Pallas kernels for 0%

commit v1 on v0

v1 whole, which is shorter than its diff:
```python
import functools

import jax
import jax.numpy as jnp
from jax import lax
from jax.experimental import pallas as pl
from jax.experimental.pallas import tpu as pltpu
from jax.sharding import PartitionSpec as P

MESH = pl.DeviceIdType.MESH
VMEM = pltpu.VMEM
F32 = jnp.float32
BF16 = jnp.bfloat16
CHUNK = 256
TILE = 256


def split(x):
    high = x.astype(BF16)
    low = (x - high.astype(F32)).astype(BF16)
    return jnp.concatenate([high, low], axis=1)


def one_hot(base, rows, ids):
    near = ids - base
    row = lax.broadcasted_iota(jnp.int32, (rows, ids.shape[1]), 0)
    return (row == near).astype(F32).astype(BF16)


def local_kernel(count, v, kmu, klam, mu, lam, ids, blocks, energy, terms):
    elements, width = v.shape
    size = width // 3
    rows = mu.shape[0]
    place = lax.broadcasted_iota(jnp.int32, (rows, 128), 0) * 128
    place = place + lax.broadcasted_iota(jnp.int32, (rows, 128), 1)
    live = place < count[0]
    mu_t = jnp.transpose(jnp.where(live, mu[...], 0.0))
    lam_t = jnp.transpose(jnp.where(live, lam[...], 0.0))
    total = jnp.zeros((8, size), F32)
    for g in range(elements // CHUNK):
        at = pl.ds(g * CHUNK, CHUNK)
        part = v[at, :]
        by_mu = jnp.dot(part, kmu[...], preferred_element_type=F32)
        by_lam = jnp.dot(part, klam[...], preferred_element_type=F32)
        n = CHUNK // 128
        a = jnp.concatenate([mu_t[:, g * n + i : g * n + i + 1] for i in range(n)], axis=0)
        b = jnp.concatenate([lam_t[:, g * n + i : g * n + i + 1] for i in range(n)], axis=0)
        forces = a * by_mu + b * by_lam
        work = part.astype(F32) * forces
        for c in range(3):
            cols = slice(c * size, (c + 1) * size)
            total = total + jnp.sum(work[:, cols].reshape(CHUNK // 8, 8, size), axis=0)
            terms[c, at, :] = split(forces[:, cols])
    energy[...] = jnp.sum(total, axis=0, keepdims=True)

    tiles = blocks.shape[1] // TILE

    def tile(i, carry):
        c = i // tiles
        base = lax.rem(i, tiles) * TILE
        hot = one_hot(base, TILE, ids[pl.ds(c, 1), :])
        both = jnp.dot(hot, terms[c], preferred_element_type=F32)
        blocks[c, pl.ds(base, TILE), :] = both[:, :size] + both[:, size:]
        return carry

    lax.fori_loop(0, 3 * tiles, tile, 0)


def exchange_kernel(
    share, blocks, slot_ids, parents, child_ids, energy_part,
    out, energy,
    summed, gather, arrived, child_out, child_in, wanted_in, wanted, mine, plane, column,
    share_send, share_recv, child_send, child_recv, wanted_sem, plane_send, plane_recv, column_send, column_recv,
):
    dom, level = lax.axis_index("dom"), lax.axis_index("level")
    ranks, levels = lax.axis_size("dom"), lax.axis_size("level")
    slots, each = share.shape
    half = slots // 2
    size = blocks.shape[2]
    count = blocks.shape[1]
    slab = ranks // 16
    offsets = [o + 1 for o in range(half)] + [-(o + 1) for o in range(half)]
    near = [(lax.rem(dom + off + ranks, ranks), level) for off in offsets]
    finer = (dom, lax.rem(level + 1, levels))
    coarser = (dom, lax.rem(level + levels - 1, levels))
    first = lax.rem(dom, slab) * levels + level
    z = dom // slab
    group = slab * levels
    in_plane = []
    for k in range(1, group):
        other = lax.rem(first + k, group)
        in_plane.append((z * slab + other // levels, lax.rem(other, levels)))
    depth = ranks // slab
    in_column = [(lax.rem(z + k, depth) * slab + lax.rem(dom, slab), level) for k in range(1, depth)]

    greeted = near + [finer, coarser] + in_plane + in_column
    barrier = pltpu.get_barrier_semaphore()
    for device in greeted:
        pl.semaphore_signal(barrier, inc=1, device_id=device, device_id_type=MESH)
    pl.semaphore_wait(barrier, len(greeted))

    def remote(src, dst, send, recv, device):
        return pltpu.make_async_remote_copy(
            src_ref=src, dst_ref=dst, send_sem=send, recv_sem=recv, device_id=device, device_id_type=MESH
        )

    ask = remote(parents, wanted_in, wanted_sem.at[0], wanted_sem.at[1], coarser)
    ask.start()
    plane_copies = [
        remote(energy_part, plane.at[k], plane_send, plane_recv, device) for k, device in enumerate(in_plane)
    ]
    for copy in plane_copies:
        copy.start()

    shares = []
    for c in range(3):
        for o in range(slots):
            def pick(s, carry):
                gather[c, o, pl.ds(s, 1), :] = blocks[c, pl.ds(jnp.minimum(share[o, s], count - 1), 1), :]
                return carry

            lax.fori_loop(0, each, pick, 0, unroll=True)
        for o in range(slots):
            there = (o + half) % slots
            copy = remote(gather.at[c, o], arrived.at[c, there], share_send.at[c, o], share_recv.at[c, there], near[o])
            copy.start()
            shares.append(copy)

    ask.wait()
    fetch = pltpu.make_async_copy(wanted_in, wanted, wanted_sem.at[2])
    fetch.start()
    remote(plane, plane, plane_send, plane_recv, finer).wait_recv()
    level_sum = energy_part[...] + jnp.sum(plane[...], axis=0)
    mine[...] = level_sum
    column_copies = [
        remote(mine, column.at[k], column_send, column_recv, device) for k, device in enumerate(in_column)
    ]
    for copy in column_copies:
        copy.start()
    fetch.wait()

    hot = one_hot(0, count, slot_ids[...])
    children = []
    for c in range(3):
        for o in range(slots):
            shares[c * slots + o].wait_recv()
        got = arrived[c].reshape(slots * each, size)
        both = jnp.dot(hot, split(got), preferred_element_type=F32)
        summed[c] = blocks[c] + (both[:, :size] + both[:, size:])

        def pair(h, carry):
            one = summed[c, pl.ds(wanted[0, h], 1), :]
            two = summed[c, pl.ds(wanted[1, h], 1), :]
            child_out[c, pl.ds(h, 1), :] = 0.5 * (one + two)
            return carry

        lax.fori_loop(0, wanted.shape[1], pair, 0, unroll=True)
        copy = remote(child_out.at[c], child_in.at[c], child_send.at[c], child_recv.at[c], finer)
        copy.start()
        children.append(copy)

    hangs = one_hot(0, count, child_ids[...])
    keep = 1.0 - jnp.sum(hangs.astype(F32), axis=1, keepdims=True)
    for c in range(3):
        children[c].wait_recv()
        both = jnp.dot(hangs, split(child_in[c]), preferred_element_type=F32)
        out[c] = keep * summed[c] + (both[:, :size] + both[:, size:])

    remote(column, column, column_send, column_recv, finer).wait_recv()
    everything = mine[...] + jnp.sum(column[...], axis=0)
    energy[...] = jnp.sum(everything, axis=1, keepdims=True)
    for copy in plane_copies + column_copies + shares + children:
        copy.wait_send()


def shards(
    dg_values, stiff_mu, stiff_lam, coef_mu, coef_lam, elem_count, elem_block, share_map, hang_child, hang_parent
):
    elements, width = dg_values.shape
    size = width // 3
    count = elements // 3
    in_vmem = pl.BlockSpec(memory_space=VMEM)
    in_smem = pl.BlockSpec(memory_space=pltpu.SMEM)
    blocks, energy_part = pl.pallas_call(
        local_kernel,
        out_shape=[jax.ShapeDtypeStruct((3, count, size), F32), jax.ShapeDtypeStruct((1, size), F32)],
        in_specs=[in_smem] + [in_vmem] * 6,
        out_specs=[in_vmem, in_vmem],
        scratch_shapes=[VMEM((3, elements, 2 * size), BF16)],
    )(
        elem_count, dg_values, stiff_mu, stiff_lam,
        coef_mu.reshape(-1, 128), coef_lam.reshape(-1, 128), elem_block,
    )
    slots, each = share_map.shape[1:]
    hangs = hang_child.shape[1]
    ranks, levels = lax.axis_size("dom"), lax.axis_size("level")
    group, depth = ranks // 16 * levels, 16
    sem = pltpu.SemaphoreType.DMA
    projected, energy = pl.pallas_call(
        exchange_kernel,
        out_shape=[jax.ShapeDtypeStruct((3, count, size), F32), jax.ShapeDtypeStruct((1, 1), F32)],
        in_specs=[in_smem] + [in_vmem] * 5,
        out_specs=[in_vmem, in_vmem],
        scratch_shapes=[
            VMEM((3, count, size), F32),
            VMEM((3, slots, each, size), F32),
            VMEM((3, slots, each, size), F32),
            VMEM((3, hangs, size), F32),
            VMEM((3, hangs, size), F32),
            VMEM((2, hangs), jnp.int32),
            pltpu.SMEM((2, hangs), jnp.int32),
            VMEM((1, size), F32),
            VMEM((group - 1, 1, size), F32),
            VMEM((depth - 1, 1, size), F32),
            sem((3, slots)), sem((3, slots)), sem((3,)), sem((3,)), sem((3,)), sem, sem, sem, sem,
        ],
        compiler_params=pltpu.CompilerParams(collective_id=0, has_side_effects=True),
    )(
        share_map[0], blocks, share_map.reshape(1, -1), jnp.transpose(hang_parent[0]), hang_child, energy_part,
    )
    scale = 0.5 / (width * elements * ranks * levels)
    return projected, energy[0, 0] * F32(scale)


def solution(mesh):
    both = ("dom", "level")
    placed = (
        P(both, None), P(), P(), P(both), P(both), P(both), P(None, both),
        P(both, None, None), P(both, None), P(both, None, None),
    )
    return jax.shard_map(
        shards, mesh=mesh, in_specs=placed, out_specs=(P(None, both, None), P()), check_vma=False
    )
```

time: 213 us -> 55.2 us (0.26); the launches traced: 210 us -> 55 us
  local copies, waits for them, and re-layouts: 69.3 us -> 3.98 us
  blocking collectives: 63.5 us -> 0 us
  Pallas kernels: 0 us -> 47.9 us
  starting transfers between devices: 29 us -> 0 us
  matrix products: 24.2 us -> 0 us
  other arithmetic: 13.5 us -> 0 us
  waiting for transfers between devices: 6.04 us -> 0 us
    psum x4 -> x0, blocking collectives: 63.5 us -> none  [by_axis(): return functools.reduce(lax.psum, axes, x)]
    dynamic_update_slice x6 -> x0, local copies, waits for them, and re-layouts: 49.6 us -> none  [shards(): local_blocks = lax.map(sum_blocks, (elem_block, component_forces))]
    pallas_call x0 -> x2, Pallas kernels: none -> 47.9 us  [the longest x1 34 us: shards(): pl.pallas_call(exchange_kernel, out_shape=[jax.ShapeDtypeStruct((3, count...]
    ppermute x10 -> x0, starting transfers between devices: 29 us -> none  [from_behind(): return lax.ppermute(block, axis, route)]
    dot_general x4 -> x0, matrix products: 24.2 us -> none  [the longest x3 21.6 us: sum_blocks(): jnp.dot(selector, component_part, precision=lax.Precision.HIGHEST, prefer...]
    scatter-add x1 -> x0, other arithmetic: 8.95 us -> none  [shards(): assembled = local_blocks.at[:, slot_blocks.reshape(-1), :].add(received)]
    ppermute x10 -> x0, waiting for transfers between devices: 6.04 us -> none  [from_behind(): return lax.ppermute(block, axis, route)]
    reshape x1, local copies, waits for them, and re-layouts: 6.19 us -> 1.33 us  [shards(): share_map.reshape(1, -1)]
  transfers between devices with their start and end apart: 10 -> 0, of which waited for: 2 -> 0; matrix products, arithmetic and copies ran while one was open for 44% -> 0% of each run, Pallas kernels for 0% -> 0%
where the time goes in v1:
time: 55.2 us; the launch traced here: 55 us
  Pallas kernels  47.9 us (87%)
  local copies, waits for them, and re-layouts  3.98 us (7%)
  between operations  3.05 us (6%)
    pallas_call x1, Pallas kernels, shards(): pl.pallas_call(exchange_kernel, out_shape=[jax.ShapeDtypeStruct((3, count...  34 us
    pallas_call x1, Pallas kernels, shards(): pl.pallas_call(local_kernel, out_shape=[jax.ShapeDtypeStruct((3, count, s...  13.9 us
    unnamed x1, local copies, waits for them, and re-layouts  2.65 us
    reshape x1, local copies, waits for them, and re-layouts, shards(): share_map.reshape(1, -1)  1.33 us

profile of v1, /device:TPU:1, one launch (start us, length us, event | category | flops | bytes accessed | tf_op | source)
XLA Modules:
  0.0 55.0 jit_solution(11975744633034932862)
XLA Ops:
  1.3 1.3 %reshape.17.slot_ids = s32[1,256]{1,0:T(1,128)} reshape(s32[1,8,32]{2,1,0:T(8,128)} %param.17) | data formatting | bytes 2048 | tf_op jit(solution)/shard_map/reshape | solution.py:219
  2.6 13.9 %shard_map.113 = (f32[3,1024,128]{2,1,0:T(8,128)}, f32[1,128]{1,0:T(1,128)}) custom-call(s32[1]{0:T(128)S(6)} %copy.13.count, bf16[3072,384]{1,0:T(8,128)(2,1)} %v.1, bf16[384,384]{1,0:T(8,128)(2,1)} %kmu.1, bf16[384,384]{1,0:T(8,128)(2,1)} %klam.1, f32[24,128]{1,0:T(8,128)} %bitcast.8, f32[24,128]{1,0:T(8,128)} %bitcast.9, s32[3,3072]{1,0:T(4,128)} %ids.1), custom_call_target="tpu_custom_call" | custom-call | tf_op jit(solution)/shard_map/pallas_call | solution.py:184
  16.5 34.0 %shard_map.114 = (f32[3,1024,128]{2,1,0:T(8,128)}, f32[1,1]{1,0:T(1,128)}) custom-call(s32[8,32]{1,0:T(8,128)} %bitcast.7, f32[3,1024,128]{2,1,0:T(8,128)} %get-tuple-element.6.blocks, s32[1,256]{1,0:T(1,128)} %reshape.17.slot_ids, s32[2,64]{1,0:T(2,128)} %bitcast.10, s32[1,64]{1,0:T(1,128)} %child_ids.1, f32[1,128]{1,0:T(1,128)} %get-tuple-element.7.energy_part), custom_call_target="tpu_custom_call" | custom-call | tf_op jit(solution)/shard_map/pallas_call | solution.py:199
  51.2 2.7 %copy.14 = f32[3,1024,128]{2,1,0:T(8,128)} copy(f32[3,1024,128]{2,1,0:T(8,128)} %get-tuple-element.12) | data formatting | bytes 3145728

commit v2 on v1

v2 whole, which is shorter than its diff:
```python
import jax
import jax.numpy as jnp
from jax import lax
from jax.experimental import pallas as pl
from jax.experimental.pallas import tpu as pltpu
from jax.sharding import PartitionSpec as P

MESH = pl.DeviceIdType.MESH
VMEM = pltpu.VMEM
F32 = jnp.float32
BF16 = jnp.bfloat16
CHUNK = 256
LOADS = 6
TILE = 256
PLANES = 16


def split(x):
    high = x.astype(BF16)
    low = (x - high.astype(F32)).astype(BF16)
    return jnp.concatenate([high, low], axis=1)


def one_hot(base, rows, ids):
    near = ids - base
    row = lax.broadcasted_iota(jnp.int32, (rows, ids.shape[1]), 0)
    return (row == near).astype(F32).astype(BF16)


def kernel(
    live, values_h, stiff_mu_h, stiff_lam_h, mu_h, lam_h, ids_h, share_h, parents_h, children_h,
    out, energy,
    values, stiff, mu, lam, ids, share, slots_v, parents, children, terms,
    gather, arrived, child_out, child_in, wanted_in, wanted, spark, column, plane_sum, plane,
    small_sem, stiff_sem, value_sem, share_send, share_recv, child_send, child_recv, wanted_sem,
    column_send, column_recv, plane_send, plane_recv,
):
    dom, level = lax.axis_index("dom"), lax.axis_index("level")
    ranks, levels = lax.axis_size("dom"), lax.axis_size("level")
    elements, width = values.shape
    size = width // 3
    count = out.shape[1]
    slots, each = share.shape
    half = slots // 2

    small = [
        pltpu.make_async_copy(src, dst, small_sem.at[i])
        for i, (src, dst) in enumerate(
            [
                (mu_h, mu), (lam_h, lam), (ids_h, ids), (share_h, share), (share_h, slots_v),
                (parents_h, parents), (children_h, children),
            ]
        )
    ]
    stiffs = []
    for c in range(3):
        for k, src in enumerate((stiff_mu_h, stiff_lam_h)):
            stiffs.append(
                pltpu.make_async_copy(
                    src.at[:, pl.ds(c * size, size)], stiff.at[c, :, pl.ds(k * size, size)], stiff_sem.at[c, k]
                )
            )
    step = elements // LOADS
    loads = [
        pltpu.make_async_copy(
            values_h.at[pl.ds(i * step, step), :], values.at[pl.ds(i * step, step), :], value_sem.at[i]
        )
        for i in range(LOADS)
    ]
    for copy in small[:2] + stiffs + loads + small[2:]:
        copy.start()

    offsets = [o + 1 for o in range(half)] + [-(o + 1) for o in range(half)]
    exists = [(dom + off >= 0) & (dom + off < ranks) for off in offsets]
    near = [(lax.rem(dom + off + ranks, ranks), level) for off in offsets]
    has_finer, has_coarser = level < levels - 1, level > 0
    finer = (dom, lax.rem(level + 1, levels))
    coarser = (dom, lax.rem(level + levels - 1, levels))
    slab = ranks // PLANES
    group = slab * levels
    place = lax.rem(dom, slab) * levels + level
    z = dom // slab
    in_column = [(lax.rem(z + k, PLANES) * slab + lax.rem(dom, slab), level) for k in range(1, PLANES)]
    in_plane = []
    for k in range(1, group):
        other = lax.rem(place + k, group)
        in_plane.append((z * slab + other // levels, lax.rem(other, levels)))

    barrier = pltpu.get_barrier_semaphore()

    def greet(device):
        pl.semaphore_signal(barrier, inc=1, device_id=device, device_id_type=MESH)

    greeted = jnp.int32(len(in_column) + len(in_plane))
    for device in in_column + in_plane:
        greet(device)
    for there, device in zip(exists + [has_finer, has_coarser], near + [finer, coarser]):
        pl.when(there)(lambda device=device: greet(device))
        greeted = greeted + there.astype(jnp.int32)

    def remote(src, dst, send, recv, device):
        return pltpu.make_async_remote_copy(
            src_ref=src, dst_ref=dst, send_sem=send, recv_sem=recv, device_id=device, device_id_type=MESH
        )

    for o in range(slots):
        @pl.when(jnp.logical_not(exists[o]))
        def _():
            arrived[:, (o) * each : (o + 1) * each, :] = jnp.zeros((3, each, size), F32)

    @pl.when(jnp.logical_not(has_coarser))
    def _():
        child_in[...] = jnp.zeros(child_in.shape, F32)

    for copy in small[:2]:
        copy.wait()
    at_row = lax.broadcasted_iota(jnp.int32, mu.shape, 0) * 128
    at_row = at_row + lax.broadcasted_iota(jnp.int32, mu.shape, 1)
    alive = at_row < live[0]
    mu_t = jnp.transpose(jnp.where(alive, mu[...], 0.0))
    lam_t = jnp.transpose(jnp.where(alive, lam[...], 0.0))
    for copy in stiffs:
        copy.wait()
    total = jnp.zeros((8, size), F32)
    n = CHUNK // 128
    for g in range(elements // CHUNK):
        if (g * CHUNK) % step == 0:
            loads[g * CHUNK // step].wait()
        rows = pl.ds(g * CHUNK, CHUNK)
        part = values[rows, :]
        a = jnp.concatenate([mu_t[:, g * n + i : g * n + i + 1] for i in range(n)], axis=0)
        b = jnp.concatenate([lam_t[:, g * n + i : g * n + i + 1] for i in range(n)], axis=0)
        for c in range(3):
            both = jnp.dot(part, stiff[c], preferred_element_type=F32)
            forces = a * both[:, :size] + b * both[:, size:]
            work = part[:, c * size : (c + 1) * size].astype(F32) * forces
            total = total + jnp.sum(work.reshape(CHUNK // 8, 8, size), axis=0)
            terms[c, rows, :] = split(forces)
    spark[...] = jnp.sum(total, axis=0, keepdims=True)
    for copy in small[2:]:
        copy.wait()

    pl.semaphore_wait(barrier, greeted)
    column_copies = [
        remote(spark, column.at[k], column_send, column_recv, device) for k, device in enumerate(in_column)
    ]
    for copy in column_copies:
        copy.start()
    ask = remote(parents, wanted_in, wanted_sem.at[0], wanted_sem.at[1], coarser)
    pl.when(has_coarser)(ask.start)

    shares = []
    for c in range(3):
        def tile(i, carry):
            base = pl.multiple_of(i * TILE, TILE)
            hot = one_hot(base, TILE, ids[c : c + 1, :])
            both = jnp.dot(hot, terms[c], preferred_element_type=F32)
            out[c, pl.ds(base, TILE), :] = both[:, :size] + both[:, size:]
            return carry

        lax.fori_loop(0, count // TILE, tile, 0)

        for o in range(slots):
            def pick(s, carry):
                row = jnp.minimum(share[o, s], count - 1)
                gather[c, pl.ds(o * each + s, 1), :] = out[c, pl.ds(row, 1), :]
                return carry

            lax.fori_loop(0, each, pick, 0, unroll=True)
        for o in range(slots):
            opposite = (o + half) % slots
            copy = remote(
                gather.at[c, pl.ds(o * each, each), :], arrived.at[c, pl.ds(opposite * each, each), :],
                share_send.at[c, o], share_recv.at[c, opposite], near[o],
            )
            pl.when(exists[o])(copy.start)
            shares.append(copy)

    @pl.when(has_finer)
    def _():
        ask.wait_recv()
        fetch = pltpu.make_async_copy(wanted_in, wanted, wanted_sem.at[2])
        fetch.start()
        fetch.wait()

    slot_ids = jnp.concatenate([slots_v[o : o + 1, :] for o in range(slots)], axis=1)
    hot = one_hot(0, count, slot_ids)
    sent = []
    for c in range(3):
        for o in range(slots):
            back = remote(
                gather.at[c, pl.ds(o * each, each), :], arrived.at[c, pl.ds(o * each, each), :],
                share_send.at[c, o], share_recv.at[c, o], near[o],
            )
            pl.when(exists[o])(back.wait_recv)
        both = jnp.dot(hot, split(arrived[c]), preferred_element_type=F32)
        out[c] = out[c] + (both[:, :size] + both[:, size:])
        copy = remote(child_out.at[c], child_in.at[c], child_send.at[c], child_recv.at[c], finer)
        sent.append(copy)

        @pl.when(has_finer)
        def _():
            def pair(h, carry):
                one = out[c, pl.ds(wanted[0, h], 1), :]
                two = out[c, pl.ds(wanted[1, h], 1), :]
                child_out[c, pl.ds(h, 1), :] = 0.5 * (one + two)
                return carry

            lax.fori_loop(0, wanted.shape[1], pair, 0, unroll=True)
            copy.start()

    hangs = one_hot(0, count, children[...])
    keep = 1.0 - jnp.sum(hangs.astype(F32), axis=1, keepdims=True)
    for c in range(3):
        pl.when(has_coarser)(sent[c].wait_recv)
        both = jnp.dot(hangs, split(child_in[c]), preferred_element_type=F32)
        out[c] = keep * out[c] + (both[:, :size] + both[:, size:])

    remote(column, column, column_send, column_recv, finer).wait_recv()
    plane_sum[...] = spark[...] + jnp.sum(column[...], axis=0)
    plane_copies = [
        remote(plane_sum, plane.at[k], plane_send, plane_recv, device) for k, device in enumerate(in_plane)
    ]
    for copy in plane_copies:
        copy.start()
    for copy in column_copies:
        copy.wait_send()
    for c in range(3):
        for o in range(slots):
            pl.when(exists[o])(shares[c * slots + o].wait_send)
        pl.when(has_finer)(sent[c].wait_send)
    pl.when(has_coarser)(ask.wait_send)
    remote(plane, plane, plane_send, plane_recv, finer).wait_recv()
    everything = plane_sum[...] + jnp.sum(plane[...], axis=0)
    scale = 0.5 / (width * elements * ranks * levels)
    energy[...] = jnp.sum(everything, axis=1, keepdims=True) * scale
    for copy in plane_copies:
        copy.wait_send()


def shards(
    dg_values, stiff_mu, stiff_lam, coef_mu, coef_lam, elem_count, elem_block, share_map, hang_child, hang_parent
):
    elements, width = dg_values.shape
    size = width // 3
    count = elements // 3
    slots, each = share_map.shape[1:]
    hangs = hang_child.shape[1]
    group = lax.axis_size("dom") // PLANES * lax.axis_size("level")
    rows = elements // 128
    in_hbm = pl.BlockSpec(memory_space=pltpu.HBM)
    in_vmem = pl.BlockSpec(memory_space=VMEM)
    sem = pltpu.SemaphoreType.DMA
    i32 = jnp.int32
    projected, energy = pl.pallas_call(
        kernel,
        out_shape=[jax.ShapeDtypeStruct((3, count, size), F32), jax.ShapeDtypeStruct((1, 1), F32)],
        in_specs=[pl.BlockSpec(memory_space=pltpu.SMEM)] + [in_hbm] * 9,
        out_specs=[in_vmem, in_vmem],
        scratch_shapes=[
            VMEM((elements, width), BF16),
            VMEM((3, width, 2 * size), BF16),
            VMEM((rows, 128), F32),
            VMEM((rows, 128), F32),
            VMEM((3, elements), i32),
            pltpu.SMEM((slots, each), i32),
            VMEM((slots, each), i32),
            VMEM((2, hangs), i32),
            VMEM((1, hangs), i32),
            VMEM((3, elements, 2 * size), BF16),
            VMEM((3, slots * each, size), F32),
            VMEM((3, slots * each, size), F32),
            VMEM((3, hangs, size), F32),
            VMEM((3, hangs, size), F32),
            VMEM((2, hangs), i32),
            pltpu.SMEM((2, hangs), i32),
            VMEM((1, size), F32),
            VMEM((PLANES - 1, 1, size), F32),
            VMEM((1, size), F32),
            VMEM((group - 1, 1, size), F32),
            sem((7,)), sem((3, 2)), sem((LOADS,)), sem((3, slots)), sem((3, slots)), sem((3,)), sem((3,)), sem((3,)),
            sem, sem, sem, sem,
        ],
        compiler_params=pltpu.CompilerParams(
            collective_id=0, has_side_effects=True, vmem_limit_bytes=24 * 2**20
        ),
    )(
        elem_count,
        *(
            pltpu.with_memory_space_constraint(x, pltpu.HBM)
            for x in (
                dg_values, stiff_mu, stiff_lam, coef_mu.reshape(rows, 128), coef_lam.reshape(rows, 128),
                elem_block, share_map[0], jnp.transpose(hang_parent[0]), hang_child,
            )
        ),
    )
    return projected, energy[0, 0]


def solution(mesh):
    both = ("dom", "level")
    placed = (
        P(both, None), P(), P(), P(both), P(both), P(both), P(None, both),
        P(both, None, None), P(both, None), P(both, None, None),
    )
    return jax.shard_map(
        shards, mesh=mesh, in_specs=placed, out_specs=(P(None, both, None), P()), check_vma=False
    )
```

time: 55.2 us -> 43.2 us (0.78)
  Pallas kernels: 47.9 us -> 38.9 us
  local copies, waits for them, and re-layouts: 3.98 us -> 1.15 us
    pallas_call x2 -> x1, Pallas kernels: 47.9 us -> 38.9 us  [shards(): pl.pallas_call(kernel, out_shape=[jax.ShapeDtypeStruct((3, count, size),...]
    unnamed x1, local copies, waits for them, and re-layouts: 2.65 us -> 1.15 us
    reshape x1 -> x0, local copies, waits for them, and re-layouts: 1.33 us -> none  [shards(): share_map.reshape(1, -1)]
where the time goes in v2:
time: 43.2 us; the launch traced here: 43 us
  Pallas kernels  38.9 us (90%)
  between operations  2.98 us (7%)
  local copies, waits for them, and re-layouts  1.15 us (3%)
    pallas_call x1, Pallas kernels, shards(): pl.pallas_call(kernel, out_shape=[jax.ShapeDtypeStruct((3, count, size),...  38.9 us
    unnamed x1, local copies, waits for them, and re-layouts  1.15 us

profile of v2, /device:TPU:1, one launch (start us, length us, event | category | flops | bytes accessed | tf_op | source)
XLA Modules:
  0.0 43.0 jit_solution(5240040166968816585)
XLA Ops:
  1.3 38.9 %shard_map.113 = (f32[3,1024,128]{2,1,0:T(8,128)S(1)}, f32[1,1]{1,0:T(1,128)}) custom-call(s32[1]{0:T(128)S(6)} %copy.14.live, bf16[3072,384]{1,0:T(8,128)(2,1)} %values_h.1, bf16[384,384]{1,0:T(8,128)(2,1)} %stiff_mu_h.1, bf16[384,384]{1,0:T(8,128)(2,1)} %stiff_lam_h.1, f32[24,128]{1,0:T(8,128)} %bitcast.7, f32[24,128]{1,0:T(8,128)} %bitcast.8, ...), custom_call_target="tpu_custom_call" | custom-call | tf_op jit(solution)/shard_map/pallas_call | solution.py:255
  40.2 1.1 %copy.15 = f32[3,1024,128]{2,1,0:T(8,128)} copy(f32[3,1024,128]{2,1,0:T(8,128)S(1)} %get-tuple-element.8) | data formatting | bytes 3145728

commit v3 on v2

--- a/solution.py
+++ b/solution.py
@@ -13,6 +13,7 @@
 LOADS = 6
 TILE = 256
 PLANES = 16
+FIRST = 6
 
 
 def split(x):
@@ -52,14 +53,9 @@
             ]
         )
     ]
-    stiffs = []
-    for c in range(3):
-        for k, src in enumerate((stiff_mu_h, stiff_lam_h)):
-            stiffs.append(
-                pltpu.make_async_copy(
-                    src.at[:, pl.ds(c * size, size)], stiff.at[c, :, pl.ds(k * size, size)], stiff_sem.at[c, k]
-                )
-            )
+    stiffs = [
+        pltpu.make_async_copy(src, stiff.at[k], stiff_sem.at[k]) for k, src in enumerate((stiff_mu_h, stiff_lam_h))
+    ]
     step = elements // LOADS
     loads = [
         pltpu.make_async_copy(
@@ -131,50 +127,72 @@
         a = jnp.concatenate([mu_t[:, g * n + i : g * n + i + 1] for i in range(n)], axis=0)
         b = jnp.concatenate([lam_t[:, g * n + i : g * n + i + 1] for i in range(n)], axis=0)
         for c in range(3):
-            both = jnp.dot(part, stiff[c], preferred_element_type=F32)
+            cols = slice(c * size, (c + 1) * size)
+            pair = jnp.concatenate([stiff[0, :, cols], stiff[1, :, cols]], axis=1)
+            both = jnp.dot(part, pair, preferred_element_type=F32)
             forces = a * both[:, :size] + b * both[:, size:]
-            work = part[:, c * size : (c + 1) * size].astype(F32) * forces
+            work = part[:, cols].astype(F32) * forces
             total = total + jnp.sum(work.reshape(CHUNK // 8, 8, size), axis=0)
             terms[c, rows, :] = split(forces)
     spark[...] = jnp.sum(total, axis=0, keepdims=True)
     for copy in small[2:]:
         copy.wait()
 
-    pl.semaphore_wait(barrier, greeted)
     column_copies = [
         remote(spark, column.at[k], column_send, column_recv, device) for k, device in enumerate(in_column)
     ]
-    for copy in column_copies:
-        copy.start()
     ask = remote(parents, wanted_in, wanted_sem.at[0], wanted_sem.at[1], coarser)
-    pl.when(has_coarser)(ask.start)
-
     shares = []
     for c in range(3):
-        def tile(i, carry):
-            base = pl.multiple_of(i * TILE, TILE)
-            hot = one_hot(base, TILE, ids[c : c + 1, :])
+        for o in range(slots):
+            opposite = (o + half) % slots
+            shares.append(
+                remote(
+                    gather.at[c, pl.ds(o * each, each), :], arrived.at[c, pl.ds(opposite * each, each), :],
+                    share_send.at[c, o], share_recv.at[c, opposite], near[o],
+                )
+            )
+
+    def meet():
+        pl.semaphore_wait(barrier, greeted)
+        for copy in column_copies:
+            copy.start()
+        pl.when(has_coarser)(ask.start)
+
+    def send_shares(c):
+        for o in range(slots):
+            pl.when(exists[o])(shares[c * slots + o].start)
+
+    soon = z >= FIRST
+    pl.when(soon)(meet)
+
+    def sums(c):
+        for i in range(count // TILE):
+            hot = one_hot(i * TILE, TILE, ids[c : c + 1, :])
             both = jnp.dot(hot, terms[c], preferred_element_type=F32)
-            out[c, pl.ds(base, TILE), :] = both[:, :size] + both[:, size:]
-            return carry
-
-        lax.fori_loop(0, count // TILE, tile, 0)
-
-        for o in range(slots):
-            def pick(s, carry):
+            out[c, i * TILE : (i + 1) * TILE, :] = both[:, :size] + both[:, size:]
+
+    def pick(c):
+        for o in range(slots):
+            for s in range(each):
                 row = jnp.minimum(share[o, s], count - 1)
-                gather[c, pl.ds(o * each + s, 1), :] = out[c, pl.ds(row, 1), :]
-                return carry
-
-            lax.fori_loop(0, each, pick, 0, unroll=True)
-        for o in range(slots):
-            opposite = (o + half) % slots
-            copy = remote(
-                gather.at[c, pl.ds(o * each, each), :], arrived.at[c, pl.ds(opposite * each, each), :],
-                share_send.at[c, o], share_recv.at[c, opposite], near[o],
-            )
-            pl.when(exists[o])(copy.start)
-            shares.append(copy)
+                gather[c, o * each + s : o * each + s + 1, :] = out[c, pl.ds(row, 1), :]
+
+    sums(0)
+    pick(0)
+    sums(1)
+    pl.when(soon)(lambda: send_shares(0))
+    pick(1)
+    sums(2)
+    pl.when(soon)(lambda: send_shares(1))
+    pick(2)
+    pl.when(soon)(lambda: send_shares(2))
+
+    @pl.when(jnp.logical_not(soon))
+    def _():
+        meet()
+        for c in range(3):
+            send_shares(c)
 
     @pl.when(has_finer)
     def _():
@@ -259,7 +277,7 @@
         out_specs=[in_vmem, in_vmem],
         scratch_shapes=[
             VMEM((elements, width), BF16),
-            VMEM((3, width, 2 * size), BF16),
+            VMEM((2, width, width), BF16),
             VMEM((rows, 128), F32),
             VMEM((rows, 128), F32),
             VMEM((3, elements), i32),
@@ -278,7 +296,7 @@
             VMEM((PLANES - 1, 1, size), F32),
             VMEM((1, size), F32),
             VMEM((group - 1, 1, size), F32),
-            sem((7,)), sem((3, 2)), sem((LOADS,)), sem((3, slots)), sem((3, slots)), sem((3,)), sem((3,)), sem((3,)),
+            sem((7,)), sem((2,)), sem((LOADS,)), sem((3, slots)), sem((3, slots)), sem((3,)), sem((3,)), sem((3,)),
             sem, sem, sem, sem,
         ],
         compiler_params=pltpu.CompilerParams(

time: 43.2 us -> 38.5 us (0.89)
  Pallas kernels: 38.9 us -> 34.2 us
    pallas_call x1, Pallas kernels: 38.9 us -> 34.2 us  [shards(): pl.pallas_call(kernel, out_shape=[jax.ShapeDtypeStruct((3, count, size),...]
where the time goes in v3:
time: 38.5 us; the launch traced here: 38.3 us
  Pallas kernels  34.2 us (89%)
  between operations  2.98 us (8%)
  local copies, waits for them, and re-layouts  1.15 us (3%)
    pallas_call x1, Pallas kernels, shards(): pl.pallas_call(kernel, out_shape=[jax.ShapeDtypeStruct((3, count, size),...  34.2 us
    unnamed x1, local copies, waits for them, and re-layouts  1.15 us

profile of v3, /device:TPU:1, one launch (start us, length us, event | category | flops | bytes accessed | tf_op | source)
XLA Modules:
  0.0 38.3 jit_solution(14453084706647956328)
XLA Ops:
  1.3 34.2 %shard_map.113 = (f32[3,1024,128]{2,1,0:T(8,128)S(1)}, f32[1,1]{1,0:T(1,128)}) custom-call(s32[1]{0:T(128)S(6)} %copy.14.live, bf16[3072,384]{1,0:T(8,128)(2,1)} %values_h.1, bf16[384,384]{1,0:T(8,128)(2,1)} %stiff_mu_h.1, bf16[384,384]{1,0:T(8,128)(2,1)} %stiff_lam_h.1, f32[24,128]{1,0:T(8,128)} %bitcast.7, f32[24,128]{1,0:T(8,128)} %bitcast.8, ...), custom_call_target="tpu_custom_call" | custom-call | tf_op jit(solution)/shard_map/pallas_call | solution.py:273
  35.5 1.1 %copy.15 = f32[3,1024,128]{2,1,0:T(8,128)} copy(f32[3,1024,128]{2,1,0:T(8,128)S(1)} %get-tuple-element.8) | data formatting | bytes 3145728

commit v4 on v3

--- a/solution.py
+++ b/solution.py
@@ -14,6 +14,7 @@
 TILE = 256
 PLANES = 16
 FIRST = 6
+EARLY = 3
 
 
 def split(x):
@@ -29,10 +30,10 @@
 
 
 def kernel(
-    live, values_h, stiff_mu_h, stiff_lam_h, mu_h, lam_h, ids_h, share_h, parents_h, children_h,
+    live_h, values_h, stiff_mu_h, stiff_lam_h, mu_h, lam_h, ids_h, share_h, parents_h, children_h,
     out, energy,
-    values, stiff, mu, lam, ids, share, slots_v, parents, children, terms,
-    gather, arrived, child_out, child_in, wanted_in, wanted, spark, column, plane_sum, plane,
+    live, values, stiff, mu, lam, ids, share, slots_v, parents, children, terms,
+    gather, arrived, child_out, child_in, wanted_in, wanted, hot, hangs, keep, spark, column, plane_sum, plane,
     small_sem, stiff_sem, value_sem, share_send, share_recv, child_send, child_recv, wanted_sem,
     column_send, column_recv, plane_send, plane_recv,
 ):
@@ -48,7 +49,7 @@
         pltpu.make_async_copy(src, dst, small_sem.at[i])
         for i, (src, dst) in enumerate(
             [
-                (mu_h, mu), (lam_h, lam), (ids_h, ids), (share_h, share), (share_h, slots_v),
+                (live_h, live), (mu_h, mu), (lam_h, lam), (ids_h, ids), (share_h, share), (share_h, slots_v),
                 (parents_h, parents), (children_h, children),
             ]
         )
@@ -63,7 +64,7 @@
         )
         for i in range(LOADS)
     ]
-    for copy in small[:2] + stiffs + loads + small[2:]:
+    for copy in small[:3] + stiffs + loads + small[3:]:
         copy.start()
 
     offsets = [o + 1 for o in range(half)] + [-(o + 1) for o in range(half)]
@@ -76,7 +77,8 @@
     group = slab * levels
     place = lax.rem(dom, slab) * levels + level
     z = dom // slab
-    in_column = [(lax.rem(z + k, PLANES) * slab + lax.rem(dom, slab), level) for k in range(1, PLANES)]
+    steps = sorted(range(1, PLANES), key=lambda k: abs(k - PLANES // 2))
+    in_column = [(lax.rem(z + k, PLANES) * slab + lax.rem(dom, slab), level) for k in steps]
     in_plane = []
     for k in range(1, group):
         other = lax.rem(place + k, group)
@@ -87,9 +89,13 @@
     def greet(device):
         pl.semaphore_signal(barrier, inc=1, device_id=device, device_id_type=MESH)
 
-    greeted = jnp.int32(len(in_column) + len(in_plane))
-    for device in in_column + in_plane:
+    early = z < EARLY
+    ahead = [lax.rem(z + k, PLANES) < EARLY for k in steps]
+    for device in in_plane:
         greet(device)
+    for other, device in zip(ahead, in_column):
+        pl.when(early == other)(lambda device=device: greet(device))
+    greeted = jnp.int32(len(in_plane)) + jnp.where(early, EARLY - 1, PLANES - 1)
     for there, device in zip(exists + [has_finer, has_coarser], near + [finer, coarser]):
         pl.when(there)(lambda device=device: greet(device))
         greeted = greeted + there.astype(jnp.int32)
@@ -108,11 +114,11 @@
     def _():
         child_in[...] = jnp.zeros(child_in.shape, F32)
 
-    for copy in small[:2]:
+    for copy in small[:3]:
         copy.wait()
     at_row = lax.broadcasted_iota(jnp.int32, mu.shape, 0) * 128
     at_row = at_row + lax.broadcasted_iota(jnp.int32, mu.shape, 1)
-    alive = at_row < live[0]
+    alive = at_row < live[0, 0]
     mu_t = jnp.transpose(jnp.where(alive, mu[...], 0.0))
     lam_t = jnp.transpose(jnp.where(alive, lam[...], 0.0))
     for copy in stiffs:
@@ -135,7 +141,7 @@
             total = total + jnp.sum(work.reshape(CHUNK // 8, 8, size), axis=0)
             terms[c, rows, :] = split(forces)
     spark[...] = jnp.sum(total, axis=0, keepdims=True)
-    for copy in small[2:]:
+    for copy in small[3:]:
         copy.wait()
 
     column_copies = [
@@ -155,15 +161,32 @@
 
     def meet():
         pl.semaphore_wait(barrier, greeted)
-        for copy in column_copies:
+        for other, copy in zip(ahead, column_copies):
+            pl.when(jnp.logical_not(early) | other)(copy.start)
+        for other, device in zip(ahead, in_column):
+            pl.when(early != other)(lambda device=device: greet(device))
+        pl.when(has_coarser)(ask.start)
+
+    def meet_far():
+        pl.semaphore_wait(barrier, PLANES - EARLY)
+        for other, copy in zip(ahead, column_copies):
+            pl.when(jnp.logical_not(other))(copy.start)
+
+    def send_shares(c):
+        for o in range(slots):
+            pl.when(exists[o])(shares[c * slots + o].start)
+
+    plane_copies = [
+        remote(plane_sum, plane.at[k], plane_send, plane_recv, device) for k, device in enumerate(in_plane)
+    ]
+
+    def pass_energy():
+        remote(column, column, column_send, column_recv, finer).wait_recv()
+        plane_sum[...] = spark[...] + jnp.sum(column[...], axis=0)
+        for copy in plane_copies:
             copy.start()
-        pl.when(has_coarser)(ask.start)
-
-    def send_shares(c):
-        for o in range(slots):
-            pl.when(exists[o])(shares[c * slots + o].start)
-
-    soon = z >= FIRST
+
+    soon = early | (z >= FIRST)
     pl.when(soon)(meet)
 
     def sums(c):
@@ -188,6 +211,12 @@
     pick(2)
     pl.when(soon)(lambda: send_shares(2))
 
+    slot_ids = jnp.concatenate([slots_v[o : o + 1, :] for o in range(slots)], axis=1)
+    hot[...] = one_hot(0, count, slot_ids)
+    chosen = one_hot(0, count, children[...])
+    hangs[...] = chosen
+    keep[...] = jnp.broadcast_to(1.0 - jnp.sum(chosen.astype(F32), axis=1, keepdims=True), keep.shape)
+
     @pl.when(jnp.logical_not(soon))
     def _():
         meet()
@@ -201,8 +230,6 @@
         fetch.start()
         fetch.wait()
 
-    slot_ids = jnp.concatenate([slots_v[o : o + 1, :] for o in range(slots)], axis=1)
-    hot = one_hot(0, count, slot_ids)
     sent = []
     for c in range(3):
         for o in range(slots):
@@ -211,7 +238,7 @@
                 share_send.at[c, o], share_recv.at[c, o], near[o],
             )
             pl.when(exists[o])(back.wait_recv)
-        both = jnp.dot(hot, split(arrived[c]), preferred_element_type=F32)
+        both = jnp.dot(hot[...], split(arrived[c]), preferred_element_type=F32)
         out[c] = out[c] + (both[:, :size] + both[:, size:])
         copy = remote(child_out.at[c], child_in.at[c], child_send.at[c], child_recv.at[c], finer)
         sent.append(copy)
@@ -227,20 +254,14 @@
             lax.fori_loop(0, wanted.shape[1], pair, 0, unroll=True)
             copy.start()
 
-    hangs = one_hot(0, count, children[...])
-    keep = 1.0 - jnp.sum(hangs.astype(F32), axis=1, keepdims=True)
+    pl.when(early)(meet_far)
+    pass_energy()
+
     for c in range(3):
         pl.when(has_coarser)(sent[c].wait_recv)
-        both = jnp.dot(hangs, split(child_in[c]), preferred_element_type=F32)
-        out[c] = keep * out[c] + (both[:, :size] + both[:, size:])
-
-    remote(column, column, column_send, column_recv, finer).wait_recv()
-    plane_sum[...] = spark[...] + jnp.sum(column[...], axis=0)
-    plane_copies = [
-        remote(plane_sum, plane.at[k], plane_send, plane_recv, device) for k, device in enumerate(in_plane)
-    ]
-    for copy in plane_copies:
-        copy.start()
+        both = jnp.dot(hangs[...], split(child_in[c]), preferred_element_type=F32)
+        out[c] = keep[...] * out[c] + (both[:, :size] + both[:, size:])
+
     for copy in column_copies:
         copy.wait_send()
     for c in range(3):
@@ -273,9 +294,10 @@
     projected, energy = pl.pallas_call(
         kernel,
         out_shape=[jax.ShapeDtypeStruct((3, count, size), F32), jax.ShapeDtypeStruct((1, 1), F32)],
-        in_specs=[pl.BlockSpec(memory_space=pltpu.SMEM)] + [in_hbm] * 9,
+        in_specs=[in_hbm] * 10,
         out_specs=[in_vmem, in_vmem],
         scratch_shapes=[
+            pltpu.SMEM((1, 1), i32),
             VMEM((elements, width), BF16),
             VMEM((2, width, width), BF16),
             VMEM((rows, 128), F32),
@@ -292,18 +314,21 @@
             VMEM((3, hangs, size), F32),
             VMEM((2, hangs), i32),
             pltpu.SMEM((2, hangs), i32),
+            VMEM((count, slots * each), BF16),
+            VMEM((count, hangs), BF16),
+            VMEM((count, size), F32),
             VMEM((1, size), F32),
             VMEM((PLANES - 1, 1, size), F32),
             VMEM((1, size), F32),
             VMEM((group - 1, 1, size), F32),
-            sem((7,)), sem((2,)), sem((LOADS,)), sem((3, slots)), sem((3, slots)), sem((3,)), sem((3,)), sem((3,)),
+            sem((8,)), sem((2,)), sem((LOADS,)), sem((3, slots)), sem((3, slots)), sem((3,)), sem((3,)), sem((3,)),
             sem, sem, sem, sem,
         ],
         compiler_params=pltpu.CompilerParams(
             collective_id=0, has_side_effects=True, vmem_limit_bytes=24 * 2**20
         ),
     )(
-        elem_count,
+        elem_count.reshape(1, 1),
         *(
             pltpu.with_memory_space_constraint(x, pltpu.HBM)
             for x in (

time: 38.5 us -> 36.1 us (0.938)
  Pallas kernels: 34.2 us -> 31.8 us
    pallas_call x1, Pallas kernels: 34.2 us -> 31.8 us  [shards(): pl.pallas_call(kernel, out_shape=[jax.ShapeDtypeStruct((3, count, size),...]
where the time goes in v4:
time: 36.1 us; the launch traced here: 35.9 us
  Pallas kernels  31.8 us (88%)
  between operations  2.98 us (8%)
  local copies, waits for them, and re-layouts  1.15 us (3%)
    pallas_call x1, Pallas kernels, shards(): pl.pallas_call(kernel, out_shape=[jax.ShapeDtypeStruct((3, count, size),...  31.8 us
    unnamed x1, local copies, waits for them, and re-layouts  1.15 us

profile of v4, /device:TPU:1, one launch (start us, length us, event | category | flops | bytes accessed | tf_op | source)
XLA Modules:
  0.0 35.9 jit_solution(6519444847633799986)
XLA Ops:
  1.3 31.8 %shard_map.113 = (f32[3,1024,128]{2,1,0:T(8,128)S(1)}, f32[1,1]{1,0:T(1,128)}) custom-call(s32[1,1]{1,0:T(1,128)} %bitcast.8.live_h, bf16[3072,384]{1,0:T(8,128)(2,1)} %values_h.1, bf16[384,384]{1,0:T(8,128)(2,1)} %stiff_mu_h.1, bf16[384,384]{1,0:T(8,128)(2,1)} %stiff_lam_h.1, f32[24,128]{1,0:T(8,128)} %bitcast.9, f32[24,128]{1,0:T(8,128)} %bitcast.10, ...), custom_call_target="tpu_custom_call" | custom-call | tf_op jit(solution)/shard_map/pallas_call | solution.py:294
  33.1 1.1 %copy.15 = f32[3,1024,128]{2,1,0:T(8,128)} copy(f32[3,1024,128]{2,1,0:T(8,128)S(1)} %get-tuple-element.8) | data formatting | bytes 3145728

commit v5 on v4

--- a/solution.py
+++ b/solution.py
@@ -10,7 +10,7 @@
 F32 = jnp.float32
 BF16 = jnp.bfloat16
 CHUNK = 256
-LOADS = 6
+LOADS = (4, 8)
 TILE = 256
 PLANES = 16
 FIRST = 6
@@ -57,12 +57,12 @@
     stiffs = [
         pltpu.make_async_copy(src, stiff.at[k], stiff_sem.at[k]) for k, src in enumerate((stiff_mu_h, stiff_lam_h))
     ]
-    step = elements // LOADS
+    starts = [sum(LOADS[:i]) * CHUNK for i in range(len(LOADS))]
     loads = [
         pltpu.make_async_copy(
-            values_h.at[pl.ds(i * step, step), :], values.at[pl.ds(i * step, step), :], value_sem.at[i]
+            values_h.at[pl.ds(start, n * CHUNK), :], values.at[pl.ds(start, n * CHUNK), :], value_sem.at[i]
         )
-        for i in range(LOADS)
+        for i, (start, n) in enumerate(zip(starts, LOADS))
     ]
     for copy in small[:3] + stiffs + loads + small[3:]:
         copy.start()
@@ -126,8 +126,8 @@
     total = jnp.zeros((8, size), F32)
     n = CHUNK // 128
     for g in range(elements // CHUNK):
-        if (g * CHUNK) % step == 0:
-            loads[g * CHUNK // step].wait()
+        if g * CHUNK in starts:
+            loads[starts.index(g * CHUNK)].wait()
         rows = pl.ds(g * CHUNK, CHUNK)
         part = values[rows, :]
         a = jnp.concatenate([mu_t[:, g * n + i : g * n + i + 1] for i in range(n)], axis=0)
@@ -321,7 +321,7 @@
             VMEM((PLANES - 1, 1, size), F32),
             VMEM((1, size), F32),
             VMEM((group - 1, 1, size), F32),
-            sem((8,)), sem((2,)), sem((LOADS,)), sem((3, slots)), sem((3, slots)), sem((3,)), sem((3,)), sem((3,)),
+            sem((8,)), sem((2,)), sem((len(LOADS),)), sem((3, slots)), sem((3, slots)), sem((3,)), sem((3,)), sem((3,)),
             sem, sem, sem, sem,
         ],
         compiler_params=pltpu.CompilerParams(

time: 36.1 us -> 35 us (0.970)
  Pallas kernels: 31.8 us -> 30.7 us
    pallas_call x1, Pallas kernels: 31.8 us -> 30.7 us  [shards(): pl.pallas_call(kernel, out_shape=[jax.ShapeDtypeStruct((3, count, size),...]
where the time goes in v5:
time: 35 us; the launch traced here: 34.9 us
  Pallas kernels  30.7 us (88%)
  between operations  2.98 us (9%)
  local copies, waits for them, and re-layouts  1.15 us (3%)
    pallas_call x1, Pallas kernels, shards(): pl.pallas_call(kernel, out_shape=[jax.ShapeDtypeStruct((3, count, size),...  30.7 us
    unnamed x1, local copies, waits for them, and re-layouts  1.15 us

profile of v5, /device:TPU:1, one launch (start us, length us, event | category | flops | bytes accessed | tf_op | source)
XLA Modules:
  0.0 34.9 jit_solution(15214507981259120853)
XLA Ops:
  1.3 30.7 %shard_map.113 = (f32[3,1024,128]{2,1,0:T(8,128)S(1)}, f32[1,1]{1,0:T(1,128)}) custom-call(s32[1,1]{1,0:T(1,128)} %bitcast.8.live_h, bf16[3072,384]{1,0:T(8,128)(2,1)} %values_h.1, bf16[384,384]{1,0:T(8,128)(2,1)} %stiff_mu_h.1, bf16[384,384]{1,0:T(8,128)(2,1)} %stiff_lam_h.1, f32[24,128]{1,0:T(8,128)} %bitcast.9, f32[24,128]{1,0:T(8,128)} %bitcast.10, ...), custom_call_target="tpu_custom_call" | custom-call | tf_op jit(solution)/shard_map/pallas_call | solution.py:294
  32.0 1.1 %copy.15 = f32[3,1024,128]{2,1,0:T(8,128)} copy(f32[3,1024,128]{2,1,0:T(8,128)S(1)} %get-tuple-element.8) | data formatting | bytes 3145728
